TPU v7x, 32 devices: a whole 2x2x4 slice. The times are simulated.
32 devices in a mesh: grp: 8 (over y, x, core), inner: 4 (over z).
Axes of the slice: x: 2, y: 2, z: 4, core: 2. Of those that a mesh axis runs over, the one named last changes fastest.
Arguments:
- amplitudes: bfloat16 [16, 8, 12288], P('grp', None, 'inner'), may hold values from -6 to 6
- factors: bfloat16 [16, 2000, 12288], P('grp', 'inner'), may hold values from -0.125 to 0.125
- atom_charges: bfloat16 [16, 64, 12288], P('grp', None, 'inner'), may hold values from -0.0068359375 to 0.0068359375
- eps_occ: float32 [16, 48], P('grp'), may hold values from -1.2 to -0.3
- eps_vir: float32 [16, 256], P('grp'), may hold values from 0.1 to 1.5
- occ_count: int32 [16], P('grp'), may hold values from 24 to 48
- vir_count: int32 [16], P('grp'), may hold values from 128 to 256
- atom_list: int32 [1024], P('grp'), may hold values from 0 to 1023, each once
- positions: float32 [3, 1024], replicated, may hold values from 0 to 12
Outputs:
- refined: float32 [16, 8, 12288], P('grp', None, 'inner')
- hamiltonian: float32 [128, 8, 16], P('grp', None, 'inner')
Inputs may be any that keep to these rules, and one draw needn't show every extreme that they name: `atom_list`: every atom index appears exactly once.
All inputs are finite; a program needn't handle non-finite values.
Results may differ from a plain program's by a relative error of at most 0.022.
Values may be sent and summed in bfloat16 or wider, within the bound.
No kernel may reach another device: no remote copies, remote signals or barrier semaphores. Data moves between devices by JAX's collectives and lax.ppermute only.
A program may use at most 64 MiB of HBM per device.

v0:
```python
import jax
import jax.numpy as jnp
from jax import lax
from jax.sharding import PartitionSpec as P

NVIR = 256
STATES = 8
epsilon = 1e-06


def coupling_block(
    group_charges, own_xyz, own_ids, energies, in_charges, in_xyz, slice_rows, inner_pos, monomers
):
    count = in_charges.shape[0]
    offset = own_xyz[:, :, :, None, None] - jnp.transpose(in_xyz, (1, 0, 2))[None, :, None, :, :]
    kernel = 1.0 / jnp.sqrt(jnp.sum(offset * offset, axis=1) + 1.0)
    block = jnp.einsum(
        "csa,carb,rb->csr", group_charges, kernel, in_charges, precision=lax.Precision.HIGHEST
    )
    column = jnp.arange(count, dtype=jnp.int32)
    source = column // slice_rows
    within = inner_pos * slice_rows + column % slice_rows
    in_ids = source * monomers + within // STATES
    in_state = within % STATES
    same = own_ids[:, None, None] == in_ids[None, None, :]
    diag = jnp.arange(STATES, dtype=jnp.int32)[None, :, None] == in_state[None, None, :]
    block = jnp.where(same, jnp.where(diag, energies[:, :, None], 0.0), block)
    return block.reshape(monomers * STATES, count)


def local(
    amplitudes, factors, atom_charges, eps_occ, eps_vir, occ_count, vir_count, atom_list, positions
):
    monomers, states_here, local_pairs = amplitudes.shape
    atom_count = atom_charges.shape[1]
    inner_count = lax.axis_size("inner")
    inner_pos = lax.axis_index("inner")
    pair_index = inner_pos * local_pairs + jnp.arange(local_pairs, dtype=jnp.int32)
    occ_of = pair_index // NVIR
    vir_of = pair_index % NVIR
    active = (
        (occ_of[None, :] < occ_count[:, None]) & (vir_of[None, :] < vir_count[:, None])
    ).astype(jnp.float32)
    gap = jnp.take(eps_vir, vir_of, axis=1) - jnp.take(eps_occ, occ_of, axis=1)
    masked = amplitudes * active[:, None, :].astype(jnp.bfloat16)
    fitted = jnp.einsum(
        "cso,cqo->csq",
        lax.all_gather(masked, "inner", axis=2, tiled=True),
        factors,
        preferred_element_type=jnp.float32,
    )
    fitted_low = fitted.astype(jnp.bfloat16)
    current = masked.astype(jnp.float32)
    partial_value = (
        2.0 * jnp.einsum("csq,cqo->cso", fitted_low, factors, preferred_element_type=jnp.float32)
    ).astype(jnp.bfloat16)
    coulomb = lax.psum_scatter(partial_value, "inner", scatter_dimension=2, tiled=True).astype(
        jnp.float32
    )
    image = gap[:, None, :] * current + coulomb * active[:, None, :]
    numerator, squares = lax.psum(
        (jnp.sum(current * image, axis=2), jnp.sum(current * current, axis=2)), "inner"
    )
    energies = numerator / (squares + epsilon)
    refined = active[:, None, :] * (
        current - (image - energies[:, :, None] * current) / gap[:, None, :]
    )
    refined_low = refined.astype(jnp.bfloat16)
    partial_charges = jnp.einsum(
        "cso,cao->csa", refined_low, atom_charges, preferred_element_type=jnp.float32
    ).reshape(monomers * states_here, atom_count)
    slice_rows = monomers * states_here // inner_count
    group_charges = lax.psum(partial_charges, "inner")
    slice_charges = lax.dynamic_slice_in_dim(group_charges, inner_pos * slice_rows, slice_rows, 0)
    group_charges = group_charges.reshape(monomers, states_here, atom_count)
    own_xyz = (
        jnp.take(positions, atom_list, axis=1).reshape(3, monomers, atom_count).transpose(1, 0, 2)
    )
    slice_index = inner_pos * slice_rows + jnp.arange(slice_rows, dtype=jnp.int32)
    slice_xyz = jnp.take(own_xyz, slice_index // STATES, axis=0)
    group_pos = lax.axis_index("grp")
    groups = lax.axis_size("grp")
    own_ids = group_pos * monomers + jnp.arange(monomers, dtype=jnp.int32)
    block = coupling_block(
        group_charges,
        own_xyz,
        own_ids,
        energies,
        lax.all_gather(slice_charges, "grp", axis=0, tiled=True),
        lax.all_gather(slice_xyz, "grp", axis=0, tiled=True),
        slice_rows,
        inner_pos,
        monomers,
    )
    return (refined, block.reshape(monomers * states_here, groups, slice_rows))


def solution(mesh):
    in_specs = (
        P("grp", None, "inner"),
        P("grp", "inner", None),
        P("grp", None, "inner"),
        P("grp", None),
        P("grp", None),
        P("grp"),
        P("grp"),
        P("grp"),
        P(),
    )
    out_specs = (P("grp", None, "inner"), P("grp", None, "inner"))
    return jax.shard_map(local, mesh=mesh, in_specs=in_specs, out_specs=out_specs, check_vma=False)
```

profile of v0, /device:TPU:0, one launch (start us, length us, event | category | flops | bytes accessed | tf_op | source)
XLA Modules:
  0.0 175.4 jit_solution(12270682259931202777)
XLA Ops:
  7.3 0.8 fusion.36
  8.1 0.9 broadcast_multiply_fusion
  9.0 16.3 %all_gather.9 = bf16[2,8,12288]{2,1,0:T(8,128)(2,1)S(1)} all-gather(bf16[2,8,3072]{2,1,0:T(8,128)(2,1)S(1)} %broadcast_multiply_fusion), channel_id=1, replica_groups=mesh['grp'=8,'inner'=4] {'inner'}, dimensions={2}, use_global_device_ids=true | all-gather | bytes 491520 | tf_op jit(solution)/shard_map/all_gather | solution.py:48
  25.3 64.8 %fusion.7 = bf16[2,8,12288]{2,1,0:T(8,128)(2,1)} fusion(bf16[2,500,12288]{2,0,1:T(2,128)(2,1)} %param.10, bf16[2,8,12288]{2,1,0:T(8,128)(2,1)S(1)} %all_gather.9), kind=kOutput, calls=%fused_computation.9 | convolution fusion | flops 393617216 | bytes 25362432 | tf_op jit(solution)/shard_map/csq,cqo->cso/dot_general | solution.py:55
  90.6 10.8 %gather_fusion = f32[3072,2]{1,0:T(8,128)} fusion(f32[2,256]{0,1:T(8,128)S(1)} %copy.45, s32[3072]{0:T(1024)S(1)} %broadcast_clamp_fusion.1), kind=kCustom, calls=%fused_computation | custom fusion | bytes 61440 | tf_op jit(solution)/shard_map/jit(_take)/gather | solution.py:44
  101.4 10.8 %gather_fusion.1 = f32[3072,2]{1,0:T(8,128)} fusion(f32[2,48]{0,1:T(8,128)S(1)} %copy.46, s32[3072]{0:T(1024)S(1)} %broadcast_clamp_fusion), kind=kCustom, calls=%fused_computation.1 | custom fusion | bytes 61440 | tf_op jit(solution)/shard_map/jit(_take)/gather | solution.py:44
  112.2 3.8 %subtract_bitcast_fusion = f32[2,3072]{0,1:T(8,128)S(1)} fusion(f32[3072,2]{1,0:T(8,128)} %gather_fusion.1, f32[3072,2]{1,0:T(8,128)} %gather_fusion, pred[3072]{0:T(1024)(128)(4,1)S(1)} %get-tuple-element.14, pred[3072]{0:T(1024)(128)(4,1)S(1)} %get-tuple-element.15), kind=kLoop, calls=%fused_computation.14 | loop fusion | flops 18432 | bytes 79872 | tf_op jit(solution)/shard_map/sub | solution.py:44
  116.0 0.5 copy.47
  116.5 0.2 copy.50
  116.7 0.6 gather_fusion.2
  117.6 0.6 gather_fusion.3
  118.2 9.2 %all_gather.10 = f32[32,3,64]{2,1,0:T(4,128)S(1)} all-gather(f32[4,3,64]{2,1,0:T(4,128)S(1)} %broadcast_select_fusion), channel_id=1, replica_groups=mesh['grp'=8,'inner'=4] {'grp'}, dimensions={0}, use_global_device_ids=true | all-gather | bytes 27648 | tf_op jit(solution)/shard_map/all_gather | solution.py:90
  127.5 1.1 multiply_reduce_fusion
  128.7 0.3 add_rsqrt_fusion
  129.0 0.6 copy-done.1
  129.6 1.1 fusion.19
  130.6 12.4 %all-reduce = (f32[2,8]{1,0:T(2,128)S(1)}, f32[2,8]{1,0:T(2,128)S(1)}) all-reduce(f32[2,8]{1,0:T(2,128)S(1)} %get-tuple-element.5, f32[2,8]{1,0:T(2,128)S(1)} %get-tuple-element.4), channel_id=1, replica_groups=mesh['grp'=8,'inner'=4] {'inner'}, use_global_device_ids=true, to_apply=%region_2.3 | all-reduce | flops 32 | bytes 256 | tf_op jit(solution)/shard_map/psum | solution.py:61
  143.1 1.0 fusion.22
  144.1 0.3 convolution_bitcast_fusion
  144.4 8.5 %psum.23 = f32[16,64]{1,0:T(8,128)S(1)} all-reduce(f32[16,64]{1,0:T(8,128)S(1)} %convolution_bitcast_fusion), channel_id=1, replica_groups=mesh['grp'=8,'inner'=4] {'inner'}, use_global_device_ids=true, to_apply=%region_5.6 | all-reduce | flops 1024 | bytes 8192 | tf_op jit(solution)/shard_map/psum | solution.py:73
  152.9 8.9 %all-gather = f32[8,4,64]{2,1,0:T(4,128)S(1)} all-gather(f32[1,4,64]{2,1,0:T(4,128)S(1)} %dynamic-slice_bitcast_fusion), channel_id=1, replica_groups=mesh['grp'=8,'inner'=4] {'grp'}, dimensions={0}, use_global_device_ids=true | all-gather | bytes 9216 | tf_op jit(solution)/shard_map/all_gather | solution.py:89
  161.8 5.8 %fusion.10 = f32[32,1,2,64]{3,1,2,0:T(1,128)S(1)} fusion(f32[32,64,1,1]{1,2,3,0:T(1,128)S(1)} %bitcast.34, f32[2,64,32,64]{3,2,1,0:T(8,128)S(1)} %add_rsqrt_fusion), kind=kOutput, calls=%fused_computation.11 | convolution fusion | flops 3145728 | bytes 1073152 | tf_op jit(solution)/shard_map/csa,carb,rb->csr/dot_general | solution.py:17
  167.6 0.2 convolution_select_fusion
  167.9 0.7 reshape_reshape.3
  (41 shorter events, 1.0 us)
Async XLA Ops:
  7.2 136.9 %copy-start = (bf16[2,64,3072]{2,1,0:T(8,128)(2,1)S(1)}, bf16[2,64,3072]{2,1,0:T(8,128)(2,1)}, u32[]{:S(2)}) copy-start(bf16[2,64,3072]{2,1,0:T(8,128)(2,1)} %param.11) | copy-start | bytes 2359300
  7.2 121.8 %reduce-scatter.2.cloned.1.call-start = ((), (), s32[]{:S(2)}) async-start(), calls=%async_computation.1 | async-start | bytes 491520 | tf_op jit(solution)/shard_map/reduce_scatter | solution.py:57
  25.3 65.0 %copy-start.6 = (s32[128]{0:T(128)S(1)}, s32[128]{0:T(128)}, u32[]{:S(2)}) copy-start(s32[128]{0:T(128)} %param.16) | copy-start | bytes 1540
  25.3 65.1 %copy-start.4 = (f32[2,256]{1,0:T(2,128)S(1)}, f32[2,256]{1,0:T(2,128)}, u32[]{:S(2)}) copy-start(f32[2,256]{1,0:T(2,128)} %param.13) | copy-start | bytes 6148
  25.3 65.2 %copy-start.5 = (f32[2,48]{1,0:T(2,128)S(1)}, f32[2,48]{1,0:T(2,128)}, u32[]{:S(2)}) copy-start(f32[2,48]{1,0:T(2,128)} %param.12) | copy-start | bytes 1156
  112.2 4.3 %copy-start.3 = (f32[3,1024]{1,0:T(4,128)S(1)}, f32[3,1024]{1,0:T(4,128)}, u32[]{:S(2)}) copy-start(f32[3,1024]{1,0:T(4,128)} %param.17) | copy-start | bytes 36868
  128.7 0.9 copy-start.1
  144.1 24.5 %copy-start.2 = (f32[2,8,3072]{2,1,0:T(8,128)}, f32[2,8,3072]{2,1,0:T(8,128)S(1)}, u32[]{:S(2)}) copy-start(f32[2,8,3072]{2,1,0:T(8,128)S(1)} %fusion.22) | copy-start | bytes 589828
Sparse Core Ops, SparseCore 0:
  90.2 22.4 reduce-scatter.1
where the time goes:
time: 176 us; the launch traced here: 175 us
  matrix products  71 us (40%)
  blocking collectives  55.3 us (31%)
  local copies, waits for them, and re-layouts  25.3 us (14%)
  between operations  14.3 us (8%)
  other arithmetic  9.37 us (5%)
    dot_general x1, matrix products, local(): jnp.einsum('csq,cqo->cso', fitted_low, factors, preferred_element_type=jn...  64.8 us
    gather x2, local copies, waits for them, and re-layouts, local(): gap = jnp.take(eps_vir, vir_of, axis=1) - jnp.take(eps_occ, occ_of, axis=1)  21.6 us
    all_gather x1, blocking collectives, local(): lax.all_gather(masked, 'inner', axis=2, tiled=True)  16.3 us
    psum x1, blocking collectives, local(): lax.psum((jnp.sum(current * image, axis=2), jnp.sum(current * current, ax...  12.4 us
    all_gather x1, blocking collectives, local(): lax.all_gather(slice_xyz, 'grp', axis=0, tiled=True)  9.24 us
    all_gather x1, blocking collectives, local(): lax.all_gather(slice_charges, 'grp', axis=0, tiled=True)  8.9 us
    psum x1, blocking collectives, local(): group_charges = lax.psum(partial_charges, 'inner')  8.5 us
    dot_general x2, matrix products, coupling_block(): jnp.einsum('csa,carb,rb->csr', group_charges, kernel, in_charges, precisi...  5.94 us
  transfers between devices with their start and end apart: 1, of which 0 were waited for; matrix products, arithmetic and copies ran while one was open for 17% of the time, Pallas kernels for 0%

commit v1 on v0

--- a/solution.py
+++ b/solution.py
@@ -6,6 +6,22 @@
 NVIR = 256
 STATES = 8
 epsilon = 1e-06
+
+
+def ring_product(shard, axis, dim, contribution):
+    size, index, span = (lax.axis_size(axis), lax.axis_index(axis), shard.shape[dim])
+    right = [(i, (i + 1) % size) for i in range(size)]
+    backward = [(i, (i - 1) % size) for i in range(size)]
+    middle = size // 2
+    from_left = from_right = shard
+    so_far = contribution(shard, index * span)
+    for lap in range(1, middle + 1):
+        from_left = lax.ppermute(from_left, axis, right)
+        if lap < size - middle:
+            from_right = lax.ppermute(from_right, axis, backward)
+            so_far = so_far + contribution(from_right, (index + lap) % size * span)
+        so_far = so_far + contribution(from_left, (index - lap) % size * span)
+    return so_far
 
 
 def coupling_block(
@@ -43,11 +59,16 @@
     ).astype(jnp.float32)
     gap = jnp.take(eps_vir, vir_of, axis=1) - jnp.take(eps_occ, occ_of, axis=1)
     masked = amplitudes * active[:, None, :].astype(jnp.bfloat16)
-    fitted = jnp.einsum(
-        "cso,cqo->csq",
-        lax.all_gather(masked, "inner", axis=2, tiled=True),
-        factors,
-        preferred_element_type=jnp.float32,
+    fitted = ring_product(
+        masked,
+        "inner",
+        2,
+        lambda own_block, at: jnp.einsum(
+            "cso,cqo->csq",
+            own_block,
+            lax.dynamic_slice_in_dim(factors, at, own_block.shape[2], axis=2),
+            preferred_element_type=jnp.float32,
+        ),
     )
     fitted_low = fitted.astype(jnp.bfloat16)
     current = masked.astype(jnp.float32)

time: 176 us -> 162 us (0.920)
  matrix products: 71 us -> 33 us
  local copies, waits for them, and re-layouts: 25.3 us -> 49.1 us
  blocking collectives: 55.3 us -> 37.5 us
  waiting for transfers between devices: 0.04 us -> 11.5 us
  starting transfers between devices: 0.04 us -> 5.29 us
    dot_general x1, matrix products: 64.8 us -> 13.4 us  [local(): jnp.einsum('csq,cqo->cso', fitted_low, factors, preferred_element_type=jn...]
    unnamed x18 -> x17, local copies, waits for them, and re-layouts: 1.06 us -> 24.7 us
    all_gather x1 -> x0, blocking collectives: 16.3 us -> none  [local(): lax.all_gather(masked, 'inner', axis=2, tiled=True)]
    dot_general x0 -> x3, matrix products: none -> 13.4 us  [local(): jnp.einsum('cso,cqo->csq', own_block, lax.dynamic_slice_in_dim(factors, a...]
    reduce_scatter x1, waiting for transfers between devices: 0.02 us -> 11.5 us  [local(): lax.psum_scatter(partial_value, 'inner', scatter_dimension=2, tiled=True)]
    ppermute x0 -> x3, starting transfers between devices: none -> 5.25 us  [the longest x2 3.16 us: ring_product(): from_left = lax.ppermute(from_left, axis, right)]
    psum x1, blocking collectives: 12.4 us -> 8.55 us  [local(): lax.psum((jnp.sum(current * image, axis=2), jnp.sum(current * current, ax...]
    psum x1, blocking collectives: 8.5 us -> 10.3 us  [local(): group_charges = lax.psum(partial_charges, 'inner')]
  transfers between devices with their start and end apart: 1 -> 4, of which waited for: 0 -> 1; matrix products, arithmetic and copies ran while one was open for 17% -> 42% of each run, Pallas kernels for 0% -> 0%
where the time goes in v1:
time: 162 us; the launch traced here: 161 us
  local copies, waits for them, and re-layouts  49.1 us (30%)
  blocking collectives  37.5 us (23%)
  matrix products  33 us (20%)
  between operations  14.3 us (9%)
  waiting for transfers between devices  11.5 us (7%)
  other arithmetic  10.7 us (7%)
  starting transfers between devices  5.29 us (3%)
    unnamed x17, local copies, waits for them, and re-layouts  24.7 us
    gather x2, local copies, waits for them, and re-layouts, local(): gap = jnp.take(eps_vir, vir_of, axis=1) - jnp.take(eps_occ, occ_of, axis=1)  21.7 us
    dot_general x3, matrix products, local(): jnp.einsum('cso,cqo->csq', own_block, lax.dynamic_slice_in_dim(factors, a...  13.4 us
    dot_general x1, matrix products, local(): jnp.einsum('csq,cqo->cso', fitted_low, factors, preferred_element_type=jn...  13.4 us
    reduce_scatter x1, waiting for transfers between devices, local(): lax.psum_scatter(partial_value, 'inner', scatter_dimension=2, tiled=True)  11.5 us
    psum x1, blocking collectives, local(): group_charges = lax.psum(partial_charges, 'inner')  10.3 us
    all_gather x1, blocking collectives, local(): lax.all_gather(slice_xyz, 'grp', axis=0, tiled=True)  9.54 us
    all_gather x1, blocking collectives, local(): lax.all_gather(slice_charges, 'grp', axis=0, tiled=True)  9.07 us
  transfers between devices with their start and end apart: 4, of which 1 were waited for; matrix products, arithmetic and copies ran while one was open for 42% of the time, Pallas kernels for 0%

profile of v1, /device:TPU:0, one launch (start us, length us, event | category | flops | bytes accessed | tf_op | source)
XLA Modules:
  0.0 161.2 jit_solution(1415939619160236500)
XLA Ops:
  7.3 0.8 fusion.49
  8.1 0.9 broadcast_multiply_fusion
  9.0 3.1 %collective-permute-start.1 = (bf16[2,8,3072]{2,1,0:T(8,128)(2,1)S(1)}, bf16[2,8,3072]{2,1,0:T(8,128)(2,1)S(1)}, u32[]{:S(2)}, u32[]{:S(2)}) collective-permute-start(bf16[2,8,3072]{2,1,0:T(8,128)(2,1)S(1)} %broadcast_multiply_fusion), channel_id=1, source_target_pairs={{0,1},{1,2},{2,3},{3,0},{4,5},{5,6},{6,7},{7,4},{8,9},{9,10},{10,1... | collective-permute-start | bytes 294920 | tf_op jit(solution)/shard_map/ppermute | solution.py:19
  12.1 2.1 %collective-permute-start = (bf16[2,8,3072]{2,1,0:T(8,128)(2,1)S(1)}, bf16[2,8,3072]{2,1,0:T(8,128)(2,1)S(1)}, u32[]{:S(2)}, u32[]{:S(2)}) collective-permute-start(bf16[2,8,3072]{2,1,0:T(8,128)(2,1)S(1)} %broadcast_multiply_fusion), channel_id=1, source_target_pairs={{0,3},{1,0},{2,1},{3,2},{4,7},{5,4},{6,5},{7,6},{8,11},{9,8},{10,9... | collective-permute-start | bytes 294920 | tf_op jit(solution)/shard_map/ppermute | solution.py:21
  14.4 0.7 compare_select_fusion.9
  15.0 0.7 compare_and_fusion.3
  15.7 24.2 %copy.54 = bf16[2,500,12288]{2,1,0:T(8,128)(2,1)} copy(bf16[2,500,12288]{2,0,1:T(2,128)(2,1)} %param.10) | data formatting | bytes 49152000 | tf_op args[1]
  40.2 10.8 %gather_fusion = f32[3072,2]{1,0:T(8,128)} fusion(f32[2,256]{0,1:T(8,128)S(1)} %copy.51, s32[3072]{0:T(1024)S(1)} %broadcast_clamp_fusion.1), kind=kCustom, calls=%fused_computation | custom fusion | bytes 61440 | tf_op jit(solution)/shard_map/jit(_take)/gather | solution.py:60
  51.1 10.8 %gather_fusion.1 = f32[3072,2]{1,0:T(8,128)} fusion(f32[2,48]{0,1:T(8,128)S(1)} %copy.52, s32[3072]{0:T(1024)S(1)} %broadcast_clamp_fusion), kind=kCustom, calls=%fused_computation.1 | custom fusion | bytes 61440 | tf_op jit(solution)/shard_map/jit(_take)/gather | solution.py:60
  61.9 3.7 %subtract_bitcast_fusion = f32[2,3072]{0,1:T(8,128)S(1)} fusion(f32[3072,2]{1,0:T(8,128)} %gather_fusion.1, f32[3072,2]{1,0:T(8,128)} %gather_fusion, pred[3072]{0:T(1024)(128)(4,1)S(1)} %get-tuple-element.14, pred[3072]{0:T(1024)(128)(4,1)S(1)} %get-tuple-element.15), kind=kLoop, calls=%fused_computation.18 | loop fusion | flops 18432 | bytes 79872 | tf_op jit(solution)/shard_map/sub | solution.py:60
  67.2 4.5 %fusion.7 = f32[2,8,500]{2,1,0:T(8,128)S(1)} fusion(bf16[2,8,3072]{2,1,0:T(8,128)(2,1)S(1)} %broadcast_multiply_fusion, bf16[2,500,12288]{2,1,0:T(8,128)(2,1)} %copy.54, s32[]{:T(128)S(6)} %select_n.217), kind=kOutput, calls=%fused_computation.13 | convolution fusion | flops 49152000 | bytes 6323460 | tf_op jit(solution)/shard_map/cso,cqo->csq/dot_general | solution.py:66
  72.4 4.5 %fusion.3 = f32[2,8,500]{2,1,0:T(8,128)S(1)} fusion(bf16[2,8,3072]{2,1,0:T(8,128)(2,1)S(1)} %collective-permute-done.1, bf16[2,500,12288]{2,1,0:T(8,128)(2,1)} %copy.54, s32[]{:T(128)S(6)} %select_n.221), kind=kOutput, calls=%fused_computation.9 | convolution fusion | flops 49152000 | bytes 6323460 | tf_op jit(solution)/shard_map/cso,cqo->csq/dot_general | solution.py:66
  76.9 4.5 %fusion.14 = f32[2,8,500]{2,1,0:T(8,128)S(1)} fusion(f32[2,8,500]{2,1,0:T(8,128)S(1)} %fusion.3, f32[2,8,500]{2,1,0:T(8,128)S(1)} %fusion.7, bf16[2,8,3072]{2,1,0:T(8,128)(2,1)S(1)} %collective-permute-done, bf16[2,500,12288]{2,1,0:T(8,128)(2,1)} %copy.54, s32[]{:T(128)S(6)} %select_n.219), kind=kOutput, calls=%fused_computation.20 | convolution fusion | flops 49168000 | bytes 6387460 | tf_op jit(solution)/shard_map/cso,cqo->csq/dot_general | solution.py:66
  81.3 13.4 %fusion = bf16[2,8,12288]{2,1,0:T(8,128)(2,1)} fusion(bf16[2,500,12288]{2,1,0:T(8,128)(2,1)} %copy.54, f32[2,8,500]{2,1,0:T(8,128)S(1)} %fusion.14, bf16[2,8,3072]{2,1,0:T(8,128)(2,1)S(1)} %collective-permute-done.2, s32[]{:T(128)S(6)} %select_n.223), kind=kOutput, calls=%fused_computation.5 | convolution fusion | flops 246169216 | bytes 31489284 | tf_op jit(solution)/shard_map/csq,cqo->cso/dot_general | solution.py:76
  94.7 9.5 %all_gather.6 = f32[32,3,64]{2,1,0:T(4,128)S(1)} all-gather(f32[4,3,64]{2,1,0:T(4,128)S(1)} %broadcast_select_fusion), channel_id=1, replica_groups=mesh['grp'=8,'inner'=4] {'grp'}, dimensions={0}, use_global_device_ids=true | all-gather | bytes 27648 | tf_op jit(solution)/shard_map/all_gather | solution.py:111
  104.3 1.1 multiply_reduce_fusion
  105.8 11.5 %reduce-scatter.2.cloned.1.call-done = bf16[2,8,3072]{2,1,0:T(8,128)(2,1)} async-done(((bf16[2,8,12288]{2,1,0:T(8,128)(2,1)}), bf16[2,8,3072]{2,1,0:T(8,128)(2,1)}) %reduce-scatter.2.cloned.1.call-update) | async-done | bytes 98320 | tf_op jit(solution)/shard_map/reduce_scatter | solution.py:78
  117.3 1.1 fusion.27
  118.3 8.5 %all-reduce = (f32[2,8]{1,0:T(2,128)S(1)}, f32[2,8]{1,0:T(2,128)S(1)}) all-reduce(f32[2,8]{1,0:T(2,128)S(1)} %get-tuple-element.5, f32[2,8]{1,0:T(2,128)S(1)} %get-tuple-element.4), channel_id=1, replica_groups=mesh['grp'=8,'inner'=4] {'inner'}, use_global_device_ids=true, to_apply=%region_2.3 | all-reduce | flops 32 | bytes 256 | tf_op jit(solution)/shard_map/psum | solution.py:82
  126.9 1.0 fusion.30
  128.2 10.3 %psum.23 = f32[16,64]{1,0:T(8,128)S(1)} all-reduce(f32[16,64]{1,0:T(8,128)S(1)} %convolution_bitcast_fusion), channel_id=1, replica_groups=mesh['grp'=8,'inner'=4] {'inner'}, use_global_device_ids=true, to_apply=%region_5.6 | all-reduce | flops 1024 | bytes 8192 | tf_op jit(solution)/shard_map/psum | solution.py:94
  138.6 9.1 %all-gather = f32[8,4,64]{2,1,0:T(4,128)S(1)} all-gather(f32[1,4,64]{2,1,0:T(4,128)S(1)} %dynamic-slice_bitcast_fusion), channel_id=1, replica_groups=mesh['grp'=8,'inner'=4] {'grp'}, dimensions={0}, use_global_device_ids=true | all-gather | bytes 9216 | tf_op jit(solution)/shard_map/all_gather | solution.py:110
  147.6 5.8 %fusion.9 = f32[32,1,2,64]{3,1,2,0:T(1,128)S(1)} fusion(f32[32,64,1,1]{1,2,3,0:T(1,128)S(1)} %bitcast.38, f32[2,64,32,64]{3,2,1,0:T(8,128)S(1)} %add_rsqrt_fusion), kind=kOutput, calls=%fused_computation.15 | convolution fusion | flops 3145728 | bytes 1073152 | tf_op jit(solution)/shard_map/csa,carb,rb->csr/dot_general | solution.py:33
  153.7 0.7 reshape_reshape.3
  (48 shorter events, 3.7 us)
Async XLA Ops:
  7.2 120.7 %copy-start = (bf16[2,64,3072]{2,1,0:T(8,128)(2,1)S(1)}, bf16[2,64,3072]{2,1,0:T(8,128)(2,1)}, u32[]{:S(2)}) copy-start(bf16[2,64,3072]{2,1,0:T(8,128)(2,1)} %param.11) | copy-start | bytes 2359300
  7.2 110.1 %reduce-scatter.2.cloned.1.call-start = ((), (), s32[]{:S(2)}) async-start(), calls=%async_computation.1 | async-start | bytes 491520 | tf_op jit(solution)/shard_map/reduce_scatter | solution.py:78
  9.0 63.4 %collective-permute-start.1 = (bf16[2,8,3072]{2,1,0:T(8,128)(2,1)S(1)}, bf16[2,8,3072]{2,1,0:T(8,128)(2,1)S(1)}, u32[]{:S(2)}, u32[]{:S(2)}) collective-permute-start(bf16[2,8,3072]{2,1,0:T(8,128)(2,1)S(1)} %broadcast_multiply_fusion), channel_id=1, source_target_pairs={{0,1},{1,2},{2,3},{3,0},{4,5},{5,6},{6,7},{7,4},{8,9},{9,10},{10,1... | collective-permute-start | bytes 294920 | tf_op jit(solution)/shard_map/ppermute | solution.py:19
  12.1 64.8 %collective-permute-start = (bf16[2,8,3072]{2,1,0:T(8,128)(2,1)S(1)}, bf16[2,8,3072]{2,1,0:T(8,128)(2,1)S(1)}, u32[]{:S(2)}, u32[]{:S(2)}) collective-permute-start(bf16[2,8,3072]{2,1,0:T(8,128)(2,1)S(1)} %broadcast_multiply_fusion), channel_id=1, source_target_pairs={{0,3},{1,0},{2,1},{3,2},{4,7},{5,4},{6,5},{7,6},{8,11},{9,8},{10,9... | collective-permute-start | bytes 294920 | tf_op jit(solution)/shard_map/ppermute | solution.py:21
  15.7 24.2 %copy-start.4 = (f32[2,256]{1,0:T(2,128)S(1)}, f32[2,256]{1,0:T(2,128)}, u32[]{:S(2)}) copy-start(f32[2,256]{1,0:T(2,128)} %param.13) | copy-start | bytes 6148
  15.7 24.4 %copy-start.5 = (f32[2,48]{1,0:T(2,128)S(1)}, f32[2,48]{1,0:T(2,128)}, u32[]{:S(2)}) copy-start(f32[2,48]{1,0:T(2,128)} %param.12) | copy-start | bytes 1156
  39.9 26.2 %copy-start.3 = (f32[3,1024]{1,0:T(4,128)S(1)}, f32[3,1024]{1,0:T(4,128)}, u32[]{:S(2)}) copy-start(f32[3,1024]{1,0:T(4,128)} %param.17) | copy-start | bytes 36868
  72.3 9.0 %collective-permute-start.2 = (bf16[2,8,3072]{2,1,0:T(8,128)(2,1)S(1)}, bf16[2,8,3072]{2,1,0:T(8,128)(2,1)S(1)}, u32[]{:S(2)}, u32[]{:S(2)}) collective-permute-start(bf16[2,8,3072]{2,1,0:T(8,128)(2,1)S(1)} %collective-permute-done.1), channel_id=1, source_target_pairs={{0,1},{1,2},{2,3},{3,0},{4,5},{5,6},{6,7},{7,4},{8,9},{9,10},{10,1... | collective-permute-start | bytes 294920 | tf_op jit(solution)/shard_map/ppermute | solution.py:19
  94.7 22.6 %copy-start.1 = (bf16[2,8,3072]{2,1,0:T(8,128)(2,1)S(1)}, bf16[2,8,3072]{2,1,0:T(8,128)(2,1)}, u32[]{:S(2)}) copy-start(bf16[2,8,3072]{2,1,0:T(8,128)(2,1)} %param.9) | copy-start | bytes 294916
  127.9 26.5 %copy-start.2 = (f32[2,8,3072]{2,1,0:T(8,128)}, f32[2,8,3072]{2,1,0:T(8,128)S(1)}, u32[]{:S(2)}) copy-start(f32[2,8,3072]{2,1,0:T(8,128)S(1)} %fusion.30) | copy-start | bytes 589828
Sparse Core Ops, SparseCore 0:
  94.8 22.3 reduce-scatter.1
